TPU v7x, 32 devices: a whole 2x2x4 slice. The times are simulated.
32 devices in a mesh: dp: 8 (over y, x, core), fsdp: 4 (over z).
Axes of the slice: x: 2, y: 2, z: 4, core: 2. Of those that a mesh axis runs over, the one named last changes fastest.
Arguments:
- tokens: bfloat16 [4096, 4096], P('dp'), may hold values from -6 to 6
- counts: int32 [8], P('dp'), may hold values from 256 to 512, as said below
- patch_index: int32 [4096], P('dp'), may hold values from 0 to 255
- clip_limit: float32 [], replicated, may hold values from 1024 to 8192
- norm_gain: float32 [4, 4096], replicated, may hold values from 0.25 to 1.75
- params: float32 [4, 4096, 4096], P(None, 'dp', 'fsdp'), may hold values from -0.09375 to 0.09375
- moments: float32 [4, 4096, 4096], P(None, 'dp', 'fsdp'), may hold values from -0.3 to 0.3
- seconds: float32 [4, 4096, 4096], P(None, 'dp', 'fsdp'), may hold values from 0.05 to 1
- gradients: float32 [4, 4096, 4096], P(None, 'dp', 'fsdp'), may hold values from -48 to 48
Outputs:
- params_new: float32 [4, 4096, 4096], P(None, 'dp', 'fsdp')
- moments_new: float32 [4, 4096, 4096], P(None, 'dp', 'fsdp')
- seconds_new: float32 [4, 4096, 4096], P(None, 'dp', 'fsdp')
- mixed: bfloat16 [4096, 4096], P('dp', 'fsdp')
Inputs may be any that keep to these rules, and one draw needn't show every extreme that they name: `counts`: at most 512, reached on some index of dp in every draw.
All inputs are finite; a program needn't handle non-finite values.
Results may differ from a plain program's by a relative error of at most 0.0095.
Values may be sent and summed in bfloat16 or wider, within the bound.
A program may use at most 192 MiB of HBM per device.

v0:
```python
import jax
import jax.numpy as jnp
from jax import lax
from jax.sharding import PartitionSpec as P

D = 4096
LAYERS = 4
GRID = 16
STEP = 40
beta_one = 0.9
beta_two = 0.95
adam_eps = 1e-08
learning_rate = 0.0024
weight_decay = 0.05
norm_eps = 1e-06


def position_code(patch_index):
    quarter = D // 4
    freqs = 1.0 / 10000.0 ** (jnp.arange(quarter, dtype=jnp.float32) / quarter)
    across = (patch_index // GRID).astype(jnp.float32)[:, None] * freqs[None, :]
    downward = (patch_index % GRID).astype(jnp.float32)[:, None] * freqs[None, :]
    return jnp.concatenate(
        [jnp.sin(across), jnp.cos(across), jnp.sin(downward), jnp.cos(downward)], axis=1
    )


def layer_norm(stream, gain_row):
    centre = jnp.mean(stream, axis=1, keepdims=True)
    shifted = stream - centre
    spread = jnp.mean(shifted * shifted, axis=1, keepdims=True)
    return (shifted * lax.rsqrt(spread + norm_eps) * gain_row[None, :]).astype(jnp.bfloat16)


def adam_update(params, moments, seconds, gradients, factor):
    clipped = gradients * factor
    moments_new = beta_one * moments + (1.0 - beta_one) * clipped
    seconds_new = beta_two * seconds + (1.0 - beta_two) * clipped * clipped
    direction = (
        moments_new
        / (1.0 - beta_one**STEP)
        / (jnp.sqrt(seconds_new / (1.0 - beta_two**STEP)) + adam_eps)
    )
    params_new = params - learning_rate * (direction + weight_decay * params)
    return (params_new, moments_new, seconds_new)


def advance(stream, branch, current, col_first, col_count):
    if current + 1 < LAYERS:
        widened = lax.all_gather(branch, "fsdp", axis=1, tiled=True)
        return stream + widened.astype(jnp.float32)
    return lax.dynamic_slice_in_dim(stream, col_first, col_count, 1) + branch.astype(jnp.float32)


def per_device(
    tokens, counts, patch_index, clip_limit, norm_gain, params, moments, seconds, gradients
):
    squares = lax.psum(jnp.sum(gradients * gradients), ("dp", "fsdp"))
    factor = jnp.minimum(1.0, clip_limit / (jnp.sqrt(squares) + 1e-06))
    params_new, moments_new, seconds_new = adam_update(params, moments, seconds, gradients, factor)
    weights = params_new.astype(jnp.bfloat16)
    tok_rows = tokens.shape[0]
    col_count = weights.shape[2]
    col_first = lax.axis_index("fsdp") * col_count
    valid = lax.broadcasted_iota(jnp.int32, (tok_rows, 1), 0) < counts[0]
    stream = jnp.where(valid, tokens.astype(jnp.float32) + position_code(patch_index), 0.0)
    gathered = lax.all_gather(weights, "dp", axis=1, tiled=True)
    for current in range(LAYERS):
        normed = layer_norm(stream, norm_gain[current])
        branch = jnp.dot(normed, gathered[current], preferred_element_type=jnp.float32).astype(
            jnp.bfloat16
        )
        stream = advance(stream, branch, current, col_first, col_count)
    mixed = jnp.where(valid, stream, 0.0).astype(jnp.bfloat16)
    return (params_new, moments_new, seconds_new, mixed)


def solution(mesh):
    in_specs = (
        P("dp", None),
        P("dp"),
        P("dp"),
        P(),
        P(),
        P(None, "dp", "fsdp"),
        P(None, "dp", "fsdp"),
        P(None, "dp", "fsdp"),
        P(None, "dp", "fsdp"),
    )
    out_specs = (
        P(None, "dp", "fsdp"),
        P(None, "dp", "fsdp"),
        P(None, "dp", "fsdp"),
        P("dp", "fsdp"),
    )
    return jax.shard_map(
        per_device, mesh=mesh, in_specs=in_specs, out_specs=out_specs, check_vma=False
    )
```

profile of v0, /device:TPU:0, one launch (start us, length us, event | category | flops | bytes accessed | tf_op | source)
XLA Modules:
  0.0 556.9 jit_solution(18285389573598532073)
XLA Ops:
  7.2 6.1 %multiply_reduce_fusion.4 = f32[]{:T(128)} fusion(f32[4,512,1024]{2,1,0:T(8,128)} %param.17), kind=kLoop, calls=%fused_computation.25 | loop fusion | flops 4194303 | bytes 8388612 | tf_op jit(solution)/shard_map/reduce_sum | solution.py:58
  14.0 42.2 %psum.7 = f32[]{:T(128)} all-reduce(f32[]{:T(128)} %multiply_reduce_fusion.4), channel_id=1, replica_groups=mesh['dp'=8,'fsdp'=4] {'dp','fsdp'}, use_global_device_ids=true, to_apply=%region_1.0 | all-reduce | flops 1 | bytes 8 | tf_op jit(solution)/shard_map/psum | solution.py:58
  57.0 20.8 %fusion.30 = (bf16[4,512,1024]{2,1,0:T(8,128)(2,1)}, f32[4,512,1024]{2,1,0:T(8,128)}, f32[4,512,1024]{2,1,0:T(8,128)}, f32[4,512,1024]{2,1,0:T(8,128)}) fusion(f32[4,512,1024]{2,1,0:T(8,128)} %param.14, f32[4,512,1024]{2,1,0:T(8,128)} %param.17, f32[]{:T(128)S(6)} %min.3, f32[4,512,1024]{2,1,0:T(8,128)} %param.15, f32[4,512,1024]{2,1,0:T(8,128)} %param.16), kind=kLoop, calls=%fused_computation.71 | loop fusion | flops 35651584 | bytes 62914564 | tf_op jit(solution)/shard_map/convert_element_type | solution.py:61
  77.8 0.2 all-gather.7.cloned.1.call-start
  78.9 14.7 %multiply_sine_fusion.1 = (f32[512,1024]{1,0:T(8,128)S(1)}, f32[512,1024]{1,0:T(8,128)S(1)}, f32[512,1024]{1,0:T(8,128)S(1)}, f32[512,1024]{1,0:T(8,128)S(1)}) fusion(f32[1024]{0:T(1024)S(1)} %negate_power_fusion, f32[512]{0:T(512)S(1)} %get-tuple-element.24, f32[512]{0:T(512)S(1)} %get-tuple-element.25), kind=kLoop, calls=%fused_computation.41 | loop fusion | flops 1048576 | bytes 8396800 | tf_op jit(solution)/shard_map/sin | solution.py:24
  93.7 1.7 fusion.28
  95.4 3.2 copy-done
  98.6 1.0 multiply_reduce_fusion.3
  99.6 139.0 %all-gather.5.cloned.1.call-done = bf16[4,4096,1024]{2,1,0:T(8,128)(2,1)} async-done(((bf16[4,512,1024]{2,1,0:T(8,128)(2,1)}), bf16[4,4096,1024]{2,1,0:T(8,128)(2,1)}) %all-gather.5.cloned.1.call-update) | async-done | bytes 33554448 | tf_op jit(solution)/shard_map/all_gather | solution.py:67
  238.6 11.3 %fusion.18 = bf16[512,1024]{1,0:T(8,128)(2,1)} fusion(bf16[4,4096,1024]{2,1,0:T(8,128)(2,1)} %all-gather.5.cloned.1.call-done, f32[512,4096]{1,0:T(8,128)} %copy-done, f32[4096]{0:T(1024)S(1)} %bitcast.33, f32[512]{0:T(512)S(1)} %add_rsqrt_fusion.3, f32[512]{0:T(512)S(1)} %broadcast_multiply_fusion.3), kind=kOutput, calls=%fused_computation.43 | convolution fusion | flops 4303880192 | bytes 17846272 | tf_op jit(solution)/shard_map/dot_general | solution.py:70
  250.0 80.8 %all-gather.7.cloned.1.call-done = bf16[512,4096]{1,0:T(8,128)(2,1)} async-done(((bf16[512,1024]{1,0:T(8,128)(2,1)}), bf16[512,4096]{1,0:T(8,128)(2,1)}) %all-gather.7.cloned.1.call-update) | async-done | bytes 4194320 | tf_op jit(solution)/shard_map/all_gather | solution.py:50
  330.8 5.6 %fusion.22 = f32[512]{0:T(512)S(1)} fusion(f32[512,4096]{1,0:T(8,128)} %copy-done, bf16[512,4096]{1,0:T(8,128)(2,1)} %all-gather.7.cloned.1.call-done), kind=kLoop, calls=%fused_computation.47 | loop fusion | flops 6290944 | bytes 12584960 | tf_op jit(solution)/shard_map/reduce_sum | solution.py:29
  336.6 5.2 multiply_reduce_fusion.2
  341.8 9.2 %fusion.19 = bf16[512,1024]{1,0:T(8,128)(2,1)} fusion(bf16[4,4096,1024]{2,1,0:T(8,128)(2,1)} %all-gather.5.cloned.1.call-done, f32[4096]{0:T(1024)S(1)} %bitcast.32, f32[512]{0:T(512)S(1)} %add_rsqrt_fusion.2, f32[512]{0:T(512)S(1)} %broadcast_multiply_fusion.2, f32[512,4096]{1,0:T(8,128)S(1)} %bitcast.29, bf16[512,4096]{1,0:T(8,128)(2,1)S(1)} %copy-done.2), kind=kOutput, calls=%fused_computation.44 | convolution fusion | flops 4308074496 | bytes 22040576 | tf_op jit(solution)/shard_map/dot_general | solution.py:70
  351.1 0.3 all-gather.11.cloned.1.call-start
  351.4 79.1 %all-gather.9.cloned.1.call-done = bf16[512,4096]{1,0:T(8,128)(2,1)} async-done(((bf16[512,1024]{1,0:T(8,128)(2,1)}), bf16[512,4096]{1,0:T(8,128)(2,1)}) %all-gather.9.cloned.1.call-update) | async-done | bytes 4194320 | tf_op jit(solution)/shard_map/all_gather | solution.py:50
  430.4 10.3 %fusion.27 = (f32[512]{0:T(512)S(1)}, f32[512,4096]{1,0:T(8,128)}) fusion(bf16[512,4096]{1,0:T(8,128)(2,1)} %all-gather.9.cloned.1.call-done, f32[512,4096]{1,0:T(8,128)} %copy-done, bf16[512,4096]{1,0:T(8,128)(2,1)} %all-gather.7.cloned.1.call-done), kind=kLoop, calls=%fused_computation.69 | loop fusion | flops 10485248 | bytes 25167872 | tf_op jit(solution)/shard_map/reduce_sum | solution.py:29
  440.8 4.5 multiply_reduce_fusion.1
  445.3 1.3 copy-done.1
  446.5 9.0 %fusion.20 = bf16[512,1024]{1,0:T(8,128)(2,1)} fusion(bf16[4,4096,1024]{2,1,0:T(8,128)(2,1)} %all-gather.5.cloned.1.call-done, f32[512,4096]{1,0:T(8,128)S(1)} %copy-done.1, f32[4096]{0:T(1024)S(1)} %bitcast.31, f32[512]{0:T(512)S(1)} %add_rsqrt_fusion.1, f32[512]{0:T(512)S(1)} %broadcast_multiply_fusion.1), kind=kOutput, calls=%fused_computation.45 | convolution fusion | flops 4303880192 | bytes 17846272 | tf_op jit(solution)/shard_map/dot_general | solution.py:70
  455.6 79.4 %all-gather.11.cloned.1.call-done = bf16[512,4096]{1,0:T(8,128)(2,1)} async-done(((bf16[512,1024]{1,0:T(8,128)(2,1)}), bf16[512,4096]{1,0:T(8,128)(2,1)}) %all-gather.11.cloned.1.call-update) | async-done | bytes 4194320 | tf_op jit(solution)/shard_map/all_gather | solution.py:50
  535.0 5.5 fusion.26
  540.5 1.0 multiply_reduce_fusion
  541.4 8.9 %select_convert_fusion = bf16[512,1024]{1,0:T(8,128)(2,1)} fusion(f32[512,4096]{1,0:T(8,128)S(1)} %get-tuple-element.5, s32[]{:T(128)S(6)} %select_n.26, bf16[4,4096,1024]{2,1,0:T(8,128)(2,1)} %all-gather.5.cloned.1.call-done, f32[4096]{0:T(1024)S(1)} %bitcast.30, f32[512]{0:T(512)S(1)} %add_rsqrt_fusion, f32[512]{0:T(512)S(1)} %broadcast_multiply_fusion, ...), kind=kOutput, calls=%fused_computation.42 | convolution fusion | flops 4305977344 | bytes 19943940 | tf_op jit(solution)/shard_map/dot_general | solution.py:70
  (33 shorter events, 0.4 us)
Async XLA Ops:
  7.2 231.5 %all-gather.5.cloned.1.call-start = ((), (), s32[]{:S(2)}) async-start(), calls=%async_computation | async-start | bytes 37748736 | tf_op jit(solution)/shard_map/all_gather | solution.py:67
  57.0 21.9 %copy-start.5 = (s32[512]{0:T(512)S(1)}, s32[512]{0:T(512)}, u32[]{:S(2)}) copy-start(s32[512]{0:T(512)} %param.11) | copy-start | bytes 6148
  77.8 253.0 %all-gather.7.cloned.1.call-start = ((), (), s32[]{:S(2)}) async-start(), calls=%async_computation.1 | async-start | bytes 5242880 | tf_op jit(solution)/shard_map/all_gather | solution.py:50
  78.0 15.6 %copy-start.3 = (bf16[512,4096]{1,0:T(8,128)(2,1)S(1)}, bf16[512,4096]{1,0:T(8,128)(2,1)}, u32[]{:S(2)}) copy-start(bf16[512,4096]{1,0:T(8,128)(2,1)} %param.9) | copy-start | bytes 12582916
  95.4 3.2 copy-start
  95.4 4.2 copy-start.4
  249.9 180.5 %all-gather.9.cloned.1.call-start = ((), (), s32[]{:S(2)}) async-start(), calls=%async_computation.2 | async-start | bytes 5242880 | tf_op jit(solution)/shard_map/all_gather | solution.py:50
  330.8 5.8 %copy-start.2 = (bf16[512,4096]{1,0:T(8,128)(2,1)S(1)}, bf16[512,4096]{1,0:T(8,128)(2,1)}, u32[]{:S(2)}) copy-start(bf16[512,4096]{1,0:T(8,128)(2,1)} %all-gather.7.cloned.1.call-done) | copy-start | bytes 12582916
  330.8 11.0 %slice-start = ((s8[8388608]{0:T(1024)(128)(4,1)}), s8[4194304]{0:T(1024)(128)(4,1)S(1)}, s32[]{:S(2)}) async-start(s8[8388608]{0:T(1024)(128)(4,1)} %bitcast.28), calls=%async_computation.4 | async-start | bytes 8388608
  336.6 5.2 slice-start.1
  351.1 183.9 %all-gather.11.cloned.1.call-start = ((), (), s32[]{:S(2)}) async-start(), calls=%async_computation.3 | async-start | bytes 5242880 | tf_op jit(solution)/shard_map/all_gather | solution.py:50
  440.7 5.8 %copy-start.1 = (f32[512,4096]{1,0:T(8,128)S(1)}, f32[512,4096]{1,0:T(8,128)}, u32[]{:S(2)}) copy-start(f32[512,4096]{1,0:T(8,128)} %get-tuple-element.7) | copy-start | bytes 25165828
Sparse Core Ops, SparseCore 0:
  77.9 160.6 all-gather.4
  250.0 80.7 all-gather.6
  351.2 79.2 all-gather.8
  455.7 79.2 all-gather.10
where the time goes:
time: 557 us
  waiting for transfers between devices  378 us (68%)
  other arithmetic  76.5 us (14%)
  blocking collectives  42.2 us (8%)
  matrix products  38.4 us (7%)
  between operations  16.1 us (3%)
    all_gather x3, waiting for transfers between devices, advance(): widened = lax.all_gather(branch, 'fsdp', axis=1, tiled=True)  239 us
    all_gather x1, waiting for transfers between devices, per_device(): gathered = lax.all_gather(weights, 'dp', axis=1, tiled=True)  139 us
    psum x1, blocking collectives, per_device(): squares = lax.psum(jnp.sum(gradients * gradients), ('dp', 'fsdp'))  42.2 us
    dot_general x4, matrix products, per_device(): jnp.dot(normed, gathered[current], preferred_element_type=jnp.float32)  38.4 us
    reduce_sum x4, other arithmetic, layer_norm(): centre = jnp.mean(stream, axis=1, keepdims=True)  23.1 us
    convert_element_type x1, other arithmetic, per_device(): weights = params_new.astype(jnp.bfloat16)  20.8 us
    sin x1, other arithmetic, position_code(): jnp.sin(across)  14.7 us
    reduce_sum x4, other arithmetic, layer_norm(): spread = jnp.mean(shifted * shifted, axis=1, keepdims=True)  11.6 us
  transfers between devices with their start and end apart: 4, of which 4 were waited for; matrix products, arithmetic and copies ran while one was open for 3% of the time, Pallas kernels for 0%

commit v1 on v0

--- a/solution.py
+++ b/solution.py
@@ -47,7 +47,14 @@
 
 def advance(stream, branch, current, col_first, col_count):
     if current + 1 < LAYERS:
-        widened = lax.all_gather(branch, "fsdp", axis=1, tiled=True)
+        size = lax.axis_size("fsdp")
+        route = [(i, (i + 1) % size) for i in range(size)]
+        blocks = [branch]
+        for far in range(1, size):
+            blocks = [lax.ppermute(blocks[0], "fsdp", route), *blocks]
+        full = jnp.concatenate(blocks, axis=1)
+        places = (lax.axis_index("fsdp") + 1) * blocks[-1].shape[1]
+        widened = jnp.roll(full, places, axis=1)
         return stream + widened.astype(jnp.float32)
     return lax.dynamic_slice_in_dim(stream, col_first, col_count, 1) + branch.astype(jnp.float32)
 

time: 557 us -> 537 us (0.964); the launches traced: 557 us -> 528 us
  waiting for transfers between devices: 378 us -> 354 us
    all_gather x3 -> x0, waiting for transfers between devices: 239 us -> none  [advance(): widened = lax.all_gather(branch, 'fsdp', axis=1, tiled=True)]
    ppermute x0 -> x9, waiting for transfers between devices: none -> 215 us  [advance(): blocks = [lax.ppermute(blocks[0], 'fsdp', route), *blocks]]
    reduce_sum x4, other arithmetic: 11.6 us -> 3.87 us  [layer_norm(): spread = jnp.mean(shifted * shifted, axis=1, keepdims=True)]
  transfers between devices with their start and end apart: 4 -> 10, of which waited for: 4 -> 10; matrix products, arithmetic and copies ran while one was open for 3% -> 3% of each run, Pallas kernels for 0% -> 0%
where the time goes in v1:
time: 537 us; the launch traced here: 528 us
  waiting for transfers between devices  354 us (66%)
  other arithmetic  72.1 us (13%)
  blocking collectives  42.2 us (8%)
  matrix products  37.7 us (7%)
  between operations  16.7 us (3%)
    ppermute x9, waiting for transfers between devices, advance(): blocks = [lax.ppermute(blocks[0], 'fsdp', route), *blocks]  215 us
    all_gather x1, waiting for transfers between devices, per_device(): gathered = lax.all_gather(weights, 'dp', axis=1, tiled=True)  139 us
    psum x1, blocking collectives, per_device(): squares = lax.psum(jnp.sum(gradients * gradients), ('dp', 'fsdp'))  42.2 us
    dot_general x4, matrix products, per_device(): jnp.dot(normed, gathered[current], preferred_element_type=jnp.float32)  37.7 us
    reduce_sum x4, other arithmetic, layer_norm(): centre = jnp.mean(stream, axis=1, keepdims=True)  26.4 us
    convert_element_type x1, other arithmetic, per_device(): weights = params_new.astype(jnp.bfloat16)  20.8 us
    sin x1, other arithmetic, position_code(): jnp.sin(across)  14.7 us
  transfers between devices with their start and end apart: 10, of which 10 were waited for; matrix products, arithmetic and copies ran while one was open for 3% of the time, Pallas kernels for 0%

profile of v1, /device:TPU:0, one launch (start us, length us, event | category | flops | bytes accessed | tf_op | source)
XLA Modules:
  0.0 528.1 jit_solution(17007816327913139336)
XLA Ops:
  7.2 6.1 %multiply_reduce_fusion.4 = f32[]{:T(128)} fusion(f32[4,512,1024]{2,1,0:T(8,128)} %param.19), kind=kLoop, calls=%fused_computation.49 | loop fusion | flops 4194303 | bytes 8388612 | tf_op jit(solution)/shard_map/reduce_sum | solution.py:65
  14.0 42.2 %psum.7 = f32[]{:T(128)} all-reduce(f32[]{:T(128)} %multiply_reduce_fusion.4), channel_id=1, replica_groups=mesh['dp'=8,'fsdp'=4] {'dp','fsdp'}, use_global_device_ids=true, to_apply=%region_1.0 | all-reduce | flops 1 | bytes 8 | tf_op jit(solution)/shard_map/psum | solution.py:65
  57.0 20.8 %fusion.51 = (bf16[4,512,1024]{2,1,0:T(8,128)(2,1)}, f32[4,512,1024]{2,1,0:T(8,128)}, f32[4,512,1024]{2,1,0:T(8,128)}, f32[4,512,1024]{2,1,0:T(8,128)}) fusion(f32[4,512,1024]{2,1,0:T(8,128)} %param.16, f32[4,512,1024]{2,1,0:T(8,128)} %param.19, f32[]{:T(128)S(6)} %min.3, f32[4,512,1024]{2,1,0:T(8,128)} %param.17, f32[4,512,1024]{2,1,0:T(8,128)} %param.18), kind=kLoop, calls=%fused_computation.116 | loop fusion | flops 35651584 | bytes 62914564 | tf_op jit(solution)/shard_map/convert_element_type | solution.py:68
  78.7 14.7 %multiply_sine_fusion.1 = (f32[512,1024]{1,0:T(8,128)S(1)}, f32[512,1024]{1,0:T(8,128)S(1)}, f32[512,1024]{1,0:T(8,128)S(1)}, f32[512,1024]{1,0:T(8,128)S(1)}) fusion(f32[1024]{0:T(1024)S(1)} %negate_power_fusion, f32[512]{0:T(512)S(1)} %get-tuple-element.27, f32[512]{0:T(512)S(1)} %get-tuple-element.28), kind=kLoop, calls=%fused_computation.86 | loop fusion | flops 1048576 | bytes 8396800 | tf_op jit(solution)/shard_map/sin | solution.py:24
  93.4 2.0 fusion.49
  95.4 3.2 copy-done
  99.6 139.0 %all-gather.2.cloned.1.call-done = bf16[4,4096,1024]{2,1,0:T(8,128)(2,1)} async-done(((bf16[4,512,1024]{2,1,0:T(8,128)(2,1)}), bf16[4,4096,1024]{2,1,0:T(8,128)(2,1)}) %all-gather.2.cloned.1.call-update) | async-done | bytes 33554448 | tf_op jit(solution)/shard_map/all_gather | solution.py:74
  238.6 10.3 %fusion.39 = bf16[512,1024]{1,0:T(8,128)(2,1)S(1)} fusion(bf16[4,4096,1024]{2,1,0:T(8,128)(2,1)} %all-gather.2.cloned.1.call-done, f32[512,4096]{1,0:T(8,128)} %copy-done, f32[4096]{0:T(1024)S(1)} %bitcast.31, f32[512]{0:T(512)S(1)} %add_rsqrt_fusion.3, f32[512]{0:T(512)S(1)} %broadcast_multiply_fusion.3), kind=kOutput, calls=%fused_computation.88 | convolution fusion | flops 4303880192 | bytes 17846272 | tf_op jit(solution)/shard_map/dot_general | solution.py:77
  248.9 1.5 collective-permute-start
  250.5 25.6 %collective-permute-done = bf16[512,1024]{1,0:T(8,128)(2,1)S(1)} collective-permute-done((bf16[512,1024]{1,0:T(8,128)(2,1)S(1)}, bf16[512,1024]{1,0:T(8,128)(2,1)S(1)}, u32[]{:S(2)}, u32[]{:S(2)}) %collective-permute-start) | collective-permute-done | bytes 1048608 | tf_op jit(solution)/shard_map/ppermute | solution.py:54
  276.1 26.2 %collective-permute-done.1 = bf16[512,1024]{1,0:T(8,128)(2,1)S(1)} collective-permute-done((bf16[512,1024]{1,0:T(8,128)(2,1)S(1)}, bf16[512,1024]{1,0:T(8,128)(2,1)S(1)}, u32[]{:S(2)}, u32[]{:S(2)}) %collective-permute-start.1) | collective-permute-done | bytes 1048608 | tf_op jit(solution)/shard_map/ppermute | solution.py:54
  302.4 25.5 %collective-permute-done.2 = bf16[512,1024]{1,0:T(8,128)(2,1)} collective-permute-done((bf16[512,1024]{1,0:T(8,128)(2,1)S(1)}, bf16[512,1024]{1,0:T(8,128)(2,1)}, u32[]{:S(2)}, u32[]{:S(2)}) %collective-permute-start.2) | collective-permute-done | bytes 1048608 | tf_op jit(solution)/shard_map/ppermute | solution.py:54
  327.9 8.8 %fusion.48 = (f32[512]{0:T(512)S(1)}, f32[512,4096]{1,0:T(8,128)S(1)}) fusion(f32[512,4096]{1,0:T(8,128)} %copy-done, s32[]{:T(128)S(6)} %select_n.42, bf16[512,1024]{1,0:T(8,128)(2,1)S(1)} %fusion.39, bf16[512,1024]{1,0:T(8,128)(2,1)S(1)} %collective-permute-done, bf16[512,1024]{1,0:T(8,128)(2,1)S(1)} %collective-permute-done.1, ...), kind=kLoop, calls=%fused_computation.114 | loop fusion | flops 37748224 | bytes 20973572 | tf_op jit(solution)/shard_map/reduce_sum | solution.py:29
  337.7 8.1 %fusion.40 = bf16[512,1024]{1,0:T(8,128)(2,1)S(1)} fusion(bf16[4,4096,1024]{2,1,0:T(8,128)(2,1)} %all-gather.2.cloned.1.call-done, f32[512,4096]{1,0:T(8,128)S(1)} %get-tuple-element.10, f32[4096]{0:T(1024)S(1)} %bitcast.30, f32[512]{0:T(512)S(1)} %add_rsqrt_fusion.2, f32[512]{0:T(512)S(1)} %broadcast_multiply_fusion.2), kind=kOutput, calls=%fused_computation.89 | convolution fusion | flops 4303880192 | bytes 17846272 | tf_op jit(solution)/shard_map/dot_general | solution.py:77
  345.9 24.5 %collective-permute-done.3 = bf16[512,1024]{1,0:T(8,128)(2,1)S(1)} collective-permute-done((bf16[512,1024]{1,0:T(8,128)(2,1)S(1)}, bf16[512,1024]{1,0:T(8,128)(2,1)S(1)}, u32[]{:S(2)}, u32[]{:S(2)}) %collective-permute-start.3) | collective-permute-done | bytes 1048608 | tf_op jit(solution)/shard_map/ppermute | solution.py:54
  370.4 23.7 %collective-permute-done.4 = bf16[512,1024]{1,0:T(8,128)(2,1)S(1)} collective-permute-done((bf16[512,1024]{1,0:T(8,128)(2,1)S(1)}, bf16[512,1024]{1,0:T(8,128)(2,1)S(1)}, u32[]{:S(2)}, u32[]{:S(2)}) %collective-permute-start.4) | collective-permute-done | bytes 1048608 | tf_op jit(solution)/shard_map/ppermute | solution.py:54
  395.1 22.0 %collective-permute-done.5 = bf16[512,1024]{1,0:T(8,128)(2,1)} collective-permute-done((bf16[512,1024]{1,0:T(8,128)(2,1)S(1)}, bf16[512,1024]{1,0:T(8,128)(2,1)}, u32[]{:S(2)}, u32[]{:S(2)}) %collective-permute-start.5) | collective-permute-done | bytes 1048608 | tf_op jit(solution)/shard_map/ppermute | solution.py:54
  417.1 7.5 %fusion.47 = (f32[512]{0:T(512)S(1)}, f32[512,4096]{1,0:T(8,128)S(1)}) fusion(f32[512,4096]{1,0:T(8,128)S(1)} %get-tuple-element.10, s32[]{:T(128)S(6)} %select_n.42, bf16[512,1024]{1,0:T(8,128)(2,1)S(1)} %fusion.40, bf16[512,1024]{1,0:T(8,128)(2,1)S(1)} %collective-permute-done.3, bf16[512,1024]{1,0:T(8,128)(2,1)} %copy-done.3, ...), kind=kLoop, calls=%fused_computation.113 | loop fusion | flops 37748224 | bytes 20973572 | tf_op jit(solution)/shard_map/reduce_sum | solution.py:29
  425.5 10.1 %fusion.41 = bf16[512,1024]{1,0:T(8,128)(2,1)S(1)} fusion(bf16[4,4096,1024]{2,1,0:T(8,128)(2,1)} %all-gather.2.cloned.1.call-done, f32[512,4096]{1,0:T(8,128)S(1)} %get-tuple-element.8, f32[4096]{0:T(1024)S(1)} %bitcast.29, f32[512]{0:T(512)S(1)} %add_rsqrt_fusion.1, f32[512]{0:T(512)S(1)} %broadcast_multiply_fusion.1), kind=kOutput, calls=%fused_computation.90 | convolution fusion | flops 4303880192 | bytes 17846272 | tf_op jit(solution)/shard_map/dot_general | solution.py:77
  435.7 23.3 %collective-permute-done.6 = bf16[512,1024]{1,0:T(8,128)(2,1)S(1)} collective-permute-done((bf16[512,1024]{1,0:T(8,128)(2,1)S(1)}, bf16[512,1024]{1,0:T(8,128)(2,1)S(1)}, u32[]{:S(2)}, u32[]{:S(2)}) %collective-permute-start.6) | collective-permute-done | bytes 1048608 | tf_op jit(solution)/shard_map/ppermute | solution.py:54
  459.0 23.1 %collective-permute-done.7 = bf16[512,1024]{1,0:T(8,128)(2,1)} collective-permute-done((bf16[512,1024]{1,0:T(8,128)(2,1)S(1)}, bf16[512,1024]{1,0:T(8,128)(2,1)}, u32[]{:S(2)}, u32[]{:S(2)}) %collective-permute-start.7) | collective-permute-done | bytes 1048608 | tf_op jit(solution)/shard_map/ppermute | solution.py:54
  482.1 20.6 %collective-permute-done.8 = bf16[512,1024]{1,0:T(8,128)(2,1)} collective-permute-done((bf16[512,1024]{1,0:T(8,128)(2,1)}, bf16[512,1024]{1,0:T(8,128)(2,1)}, u32[]{:S(2)}, u32[]{:S(2)}) %collective-permute-start.8) | collective-permute-done | bytes 1048608 | tf_op jit(solution)/shard_map/ppermute | solution.py:54
  502.7 8.2 %fusion.46 = (f32[512]{0:T(512)S(1)}, f32[512,4096]{1,0:T(8,128)S(1)}) fusion(f32[512,4096]{1,0:T(8,128)} %copy-done.1, s32[]{:T(128)S(6)} %select_n.42, bf16[512,1024]{1,0:T(8,128)(2,1)S(1)} %fusion.41, bf16[512,1024]{1,0:T(8,128)(2,1)S(1)} %collective-permute-done.6, bf16[512,1024]{1,0:T(8,128)(2,1)} %collective-permute-done.7, ...), kind=kLoop, calls=%fused_computation.112 | loop fusion | flops 37748224 | bytes 20973572 | tf_op jit(solution)/shard_map/reduce_sum | solution.py:29
  511.8 9.1 %select_convert_fusion = bf16[512,1024]{1,0:T(8,128)(2,1)} fusion(f32[512,4096]{1,0:T(8,128)S(1)} %get-tuple-element.6, s32[]{:T(128)S(6)} %select_n.35, bf16[4,4096,1024]{2,1,0:T(8,128)(2,1)} %all-gather.2.cloned.1.call-done, f32[4096]{0:T(1024)S(1)} %bitcast.28, f32[512]{0:T(512)S(1)} %add_rsqrt_fusion, f32[512]{0:T(512)S(1)} %broadcast_multiply_fusion, ...), kind=kOutput, calls=%fused_computation.87 | convolution fusion | flops 4305977344 | bytes 19943940 | tf_op jit(solution)/shard_map/dot_general | solution.py:77
  (37 shorter events, 5.2 us)
Async XLA Ops:
  7.2 231.5 %all-gather.2.cloned.1.call-start = ((), (), s32[]{:S(2)}) async-start(), calls=%async_computation | async-start | bytes 37748736 | tf_op jit(solution)/shard_map/all_gather | solution.py:74
  57.0 21.7 %copy-start.5 = (s32[512]{0:T(512)S(1)}, s32[512]{0:T(512)}, u32[]{:S(2)}) copy-start(s32[512]{0:T(512)} %param.13) | copy-start | bytes 6148
  77.8 15.6 %copy-start.2 = (bf16[512,4096]{1,0:T(8,128)(2,1)S(1)}, bf16[512,4096]{1,0:T(8,128)(2,1)}, u32[]{:S(2)}) copy-start(bf16[512,4096]{1,0:T(8,128)(2,1)} %param.11) | copy-start | bytes 12582916
  95.4 3.2 copy-start
  95.4 4.2 copy-start.4
  248.9 27.2 %collective-permute-start = (bf16[512,1024]{1,0:T(8,128)(2,1)S(1)}, bf16[512,1024]{1,0:T(8,128)(2,1)S(1)}, u32[]{:S(2)}, u32[]{:S(2)}) collective-permute-start(bf16[512,1024]{1,0:T(8,128)(2,1)S(1)} %fusion.39), channel_id=1, source_target_pairs={{0,1},{1,2},{2,3},{3,0},{4,5},{5,6},{6,7},{7,4},{8,9},{9,10},{10,1... | collective-permute-start | bytes 3145736 | tf_op jit(solution)/shard_map/ppermute | solution.py:54
  276.1 26.3 %collective-permute-start.1 = (bf16[512,1024]{1,0:T(8,128)(2,1)S(1)}, bf16[512,1024]{1,0:T(8,128)(2,1)S(1)}, u32[]{:S(2)}, u32[]{:S(2)}) collective-permute-start(bf16[512,1024]{1,0:T(8,128)(2,1)S(1)} %collective-permute-done), channel_id=1, source_target_pairs={{0,1},{1,2},{2,3},{3,0},{4,5},{5,6},{6,7},{7,4},{8,9},{9,10},{10,1... | collective-permute-start | bytes 3145736 | tf_op jit(solution)/shard_map/ppermute | solution.py:54
  302.4 25.5 %collective-permute-start.2 = (bf16[512,1024]{1,0:T(8,128)(2,1)S(1)}, bf16[512,1024]{1,0:T(8,128)(2,1)}, u32[]{:S(2)}, u32[]{:S(2)}) collective-permute-start(bf16[512,1024]{1,0:T(8,128)(2,1)S(1)} %collective-permute-done.1), channel_id=1, source_target_pairs={{0,1},{1,2},{2,3},{3,0},{4,5},{5,6},{6,7},{7,4},{8,9},{9,10},{10,1... | collective-permute-start | bytes 3145736 | tf_op jit(solution)/shard_map/ppermute | solution.py:54
  345.8 24.6 %collective-permute-start.3 = (bf16[512,1024]{1,0:T(8,128)(2,1)S(1)}, bf16[512,1024]{1,0:T(8,128)(2,1)S(1)}, u32[]{:S(2)}, u32[]{:S(2)}) collective-permute-start(bf16[512,1024]{1,0:T(8,128)(2,1)S(1)} %fusion.40), channel_id=1, source_target_pairs={{0,1},{1,2},{2,3},{3,0},{4,5},{5,6},{6,7},{7,4},{8,9},{9,10},{10,1... | collective-permute-start | bytes 3145736 | tf_op jit(solution)/shard_map/ppermute | solution.py:54
  370.4 23.7 %collective-permute-start.4 = (bf16[512,1024]{1,0:T(8,128)(2,1)S(1)}, bf16[512,1024]{1,0:T(8,128)(2,1)S(1)}, u32[]{:S(2)}, u32[]{:S(2)}) collective-permute-start(bf16[512,1024]{1,0:T(8,128)(2,1)S(1)} %collective-permute-done.3), channel_id=1, source_target_pairs={{0,1},{1,2},{2,3},{3,0},{4,5},{5,6},{6,7},{7,4},{8,9},{9,10},{10,1... | collective-permute-start | bytes 3145736 | tf_op jit(solution)/shard_map/ppermute | solution.py:54
  394.1 1.0 copy-start.3
  394.1 22.9 %collective-permute-start.5 = (bf16[512,1024]{1,0:T(8,128)(2,1)S(1)}, bf16[512,1024]{1,0:T(8,128)(2,1)}, u32[]{:S(2)}, u32[]{:S(2)}) collective-permute-start(bf16[512,1024]{1,0:T(8,128)(2,1)S(1)} %collective-permute-done.4), channel_id=1, source_target_pairs={{0,1},{1,2},{2,3},{3,0},{4,5},{5,6},{6,7},{7,4},{8,9},{9,10},{10,1... | collective-permute-start | bytes 3145736 | tf_op jit(solution)/shard_map/ppermute | solution.py:54
  424.5 11.1 %copy-start.1 = (f32[512,4096]{1,0:T(8,128)}, f32[512,4096]{1,0:T(8,128)S(1)}, u32[]{:S(2)}) copy-start(f32[512,4096]{1,0:T(8,128)S(1)} %get-tuple-element.8) | copy-start | bytes 25165828
  435.6 23.4 %collective-permute-start.6 = (bf16[512,1024]{1,0:T(8,128)(2,1)S(1)}, bf16[512,1024]{1,0:T(8,128)(2,1)S(1)}, u32[]{:S(2)}, u32[]{:S(2)}) collective-permute-start(bf16[512,1024]{1,0:T(8,128)(2,1)S(1)} %fusion.41), channel_id=1, source_target_pairs={{0,1},{1,2},{2,3},{3,0},{4,5},{5,6},{6,7},{7,4},{8,9},{9,10},{10,1... | collective-permute-start | bytes 3145736 | tf_op jit(solution)/shard_map/ppermute | solution.py:54
  459.0 23.1 %collective-permute-start.7 = (bf16[512,1024]{1,0:T(8,128)(2,1)S(1)}, bf16[512,1024]{1,0:T(8,128)(2,1)}, u32[]{:S(2)}, u32[]{:S(2)}) collective-permute-start(bf16[512,1024]{1,0:T(8,128)(2,1)S(1)} %collective-permute-done.6), channel_id=1, source_target_pairs={{0,1},{1,2},{2,3},{3,0},{4,5},{5,6},{6,7},{7,4},{8,9},{9,10},{10,1... | collective-permute-start | bytes 3145736 | tf_op jit(solution)/shard_map/ppermute | solution.py:54
  482.1 20.6 %collective-permute-start.8 = (bf16[512,1024]{1,0:T(8,128)(2,1)}, bf16[512,1024]{1,0:T(8,128)(2,1)}, u32[]{:S(2)}, u32[]{:S(2)}) collective-permute-start(bf16[512,1024]{1,0:T(8,128)(2,1)} %collective-permute-done.7), channel_id=1, source_target_pairs={{0,1},{1,2},{2,3},{3,0},{4,5},{5,6},{6,7},{7,4},{8,9},{9,10},{10,1... | collective-permute-start | bytes 3145736 | tf_op jit(solution)/shard_map/ppermute | solution.py:54
Sparse Core Ops, SparseCore 0:
  77.9 160.6 all-gather.1
